TPU v7x, 256 devices: a whole 4x4x8 slice. The times are simulated.
256 devices in a mesh: node: 8 (over y_lo, x), space: 32 (over z, y_hi, core).
Axes of the slice: x: 4, y: 4 (y_hi: 2, y_lo: 2; y = y_hi * 2 + y_lo), z: 8, core: 2. Of those that a mesh axis runs over, the one named last changes fastest.
Arguments:
- initial: float32 [2, 2048, 4096], P(None, 'space'), may hold values from 0 to 1
- sections: float32 [8, 2, 2048, 4096], P('node', None, 'space'), may hold values from 0 to 1
- feed_rate: float32 [2048, 4096], P('space'), may hold values from 0.02 to 0.12
- kill_rate: float32 [2048, 4096], P('space'), may hold values from 0.04 to 0.12
Outputs:
- new_sections: float32 [8, 2, 2048, 4096], P('node', None, 'space')
- residual_max: float32 [], replicated
All inputs are finite; a program needn't handle non-finite values.
Results may differ from a plain program's by a relative error of at most 0.000094.
Values sent between devices are 32-bit elements; how exact they have to be, the bound alone decides.
A program may use at most 64 MiB of HBM per device.

v0:
```python
import jax
import jax.numpy as jnp
import numpy as np
from jax import lax
from jax.sharding import Mesh
from jax.sharding import PartitionSpec as P

SWEEPS = 6
NODE = ("node_0", "node_1")
SPACE = ("space_0", "space_1", "space_2")
NODE_SPACE = ("node_0", "node_1", "space_0", "space_1", "space_2")


step_size = 4.0
diff_u = 1.0
diff_v = 0.5


def padded_2(array, sides, width):
    for axis, dim in sides:
        size, length = (lax.axis_size(axis), array.shape[dim])
        up = [(i, (i + 1) % size) for i in range(size)]
        down = [(j, i) for i, j in up]
        last = lax.slice_in_dim(array, length - width, length, axis=dim)
        first = lax.slice_in_dim(array, 0, width, axis=dim)
        before = lax.ppermute(last, axis, up)
        after = lax.ppermute(first, axis, down)
        array = jnp.concatenate([before, array, after], axis=dim)
    return array


def one_axis_at_a_time(array, axes):
    for axis in axes:
        array = lax.pmax(array, axis)
    return array


def radau_target(order, value):
    before = 1.0
    current = value
    previous = 1.0
    for degree in range(1, order):
        following = ((2 * degree + 1) * value * current - degree * before) / (degree + 1)
        before = current
        current = following
    previous = before
    return current - previous


def radau_table(total):
    grid_count = 20000
    roots_found = []
    left_value = -1.0
    left_target = radau_target(total, left_value)
    for step_index in range(1, grid_count):
        right_value = -1.0 + 2.0 * step_index / grid_count
        right_target = radau_target(total, right_value)
        if left_target * right_target < 0.0:
            lower = left_value
            upper = right_value
            lower_target = left_target
            for bisect_index in range(80):
                halfway = 0.5 * (lower + upper)
                halfway_target = radau_target(total, halfway)
                if lower_target * halfway_target <= 0.0:
                    upper = halfway
                else:
                    lower = halfway
                    lower_target = halfway_target
            roots_found.append(0.5 * (lower + upper))
        left_value = right_value
        left_target = right_target
    roots_found.append(1.0)
    points = [(value + 1.0) / 2.0 for value in roots_found]
    quad_rows = []
    for node_index in range(total):
        row_values = []
        for basis_index in range(total):
            coefs = [1.0]
            for other_index in range(total):
                if other_index != basis_index:
                    scale = 1.0 / (points[basis_index] - points[other_index])
                    shifted = [0.0] + coefs
                    widened = coefs + [0.0]
                    coefs = [
                        (shifted[k] - points[other_index] * widened[k]) * scale
                        for k in range(len(shifted))
                    ]
            integral = 0.0
            for power_index in range(len(coefs)):
                integral += (
                    coefs[power_index] * points[node_index] ** (power_index + 1) / (power_index + 1)
                )
            row_values.append(integral)
        quad_rows.append(row_values)
    return (np.array(points), np.array(quad_rows))


def column_pair(field):
    return jnp.roll(field, -1, 3) + jnp.roll(field, 1, 3)


def shards(initial, sections, feed_rate, kill_rate):
    local_nodes = sections.shape[0]
    total_nodes = local_nodes * lax.axis_size(NODE)
    points, quad_matrix = radau_table(total_nodes)
    points = jnp.asarray(points, jnp.float32)
    quad_matrix = jnp.asarray(quad_matrix, jnp.float32)
    first_node = lax.axis_index(NODE) * local_nodes
    diffusivity = jnp.array([diff_u, diff_v], jnp.float32).reshape(1, 2, 1, 1)
    padded = padded_2(sections, ((SPACE, 2),), 1)
    centre = padded[:, :, 1:-1]
    laplace = padded[:, :, 2:] + padded[:, :, :-2] + column_pair(centre) - 4.0 * centre
    implicit = diffusivity * laplace
    species_u = sections[:, 0]
    species_v = sections[:, 1]
    product = species_u * species_v * species_v
    reaction = jnp.stack(
        (-product + feed_rate * (1.0 - species_u), product - (feed_rate + kill_rate) * species_v),
        axis=1,
    )
    slopes = implicit + reaction
    mixed = jnp.einsum(
        "mj,jsxy->msxy",
        quad_matrix,
        lax.all_to_all(slopes, NODE, split_axis=3, concat_axis=0, tiled=True),
        precision=lax.Precision.HIGHEST,
    )
    summed = lax.all_to_all(mixed, NODE, split_axis=0, concat_axis=3, tiled=True)
    quadrature = initial[None] + step_size * summed
    residual_max = one_axis_at_a_time(jnp.max(jnp.abs(quadrature - sections)), NODE_SPACE)
    own_points = lax.dynamic_slice_in_dim(points, first_node, local_nodes, 0)
    node_step = (step_size * own_points).reshape(local_nodes, 1, 1, 1)
    right_side = quadrature - node_step * implicit
    coupling = node_step * diffusivity
    divisor = 4.0 * coupling + 1.0
    stacked = padded_2(jnp.stack((sections, right_side)), ((SPACE, 3),), SWEEPS)
    iterate = stacked[0]
    wide_side = stacked[1]
    for sweep_index in range(SWEEPS):
        middle = iterate[:, :, 1:-1]
        beside_all = iterate[:, :, 2:] + iterate[:, :, :-2] + column_pair(middle)
        margin = sweep_index + 1
        side_here = wide_side[:, :, margin : wide_side.shape[2] - margin]
        iterate = (side_here + coupling * beside_all) / divisor
    return (iterate, residual_max)


def solution(mesh):
    torus = Mesh(
        mesh.devices.reshape(2, 4, 8, 2, 2), ("node_0", "node_1", "space_0", "space_1", "space_2")
    )
    return jax.shard_map(
        shards,
        mesh=torus,
        in_specs=(P(None, SPACE, None), P(NODE, None, SPACE, None), P(SPACE, None), P(SPACE, None)),
        out_specs=(P(NODE, None, SPACE, None), P()),
        check_vma=False,
    )
```

profile of v0, /device:TPU:1, one launch (start us, length us, event | category | flops | bytes accessed | tf_op | source)
XLA Modules:
  0.0 203.4 jit_solution(11541055621538918605)
XLA Ops:
  0.6 1.1 fusion.51
  1.7 4.4 %collective-permute-start.1 = (f32[1,2,1,4096]{3,1,2,0:T(2,128)S(1)}, f32[1,2,1,4096]{3,1,2,0:T(2,128)S(1)}, u32[]{:S(2)}, u32[]{:S(2)}) collective-permute-start(f32[1,2,1,4096]{3,1,2,0:T(2,128)S(1)} %copy.76), channel_id=1, source_target_pairs={{0,1},{1,2},{2,3},{3,4},{4,5},{5,6},{6,7},{7,8},{8,9},{9,10},{10,1... | collective-permute-start | bytes 98312 | tf_op jit(solution)/shard_map/ppermute | solution.py:26
  6.3 3.1 %fusion.52 = (f32[1,2,64,4095]{3,2,1,0:T(8,128)S(1)}, f32[1,2,64,4095]{3,2,1,0:T(8,128)S(1)}) fusion(f32[1,2,64,4096]{3,2,1,0:T(8,128)} %param.8), kind=kLoop, calls=%fused_computation.80 | loop fusion | bytes 8386560 | tf_op jit(solution)/shard_map/jit(_roll_static)/slice | solution.py:100
  9.6 0.3 fusion.37
  10.0 1.4 collective-permute-done
  11.4 3.0 %maximum_add_fusion.6 = (f32[1,2,64,4096]{3,2,1,0:T(8,128)}, f32[1,2,64,4096]{3,2,1,0:T(8,128)}) fusion(f32[1,1,64,4096]{3,2,1,0:T(8,128)S(1)} %get-tuple-element.15, f32[1,1,64,4096]{3,2,1,0:T(8,128)S(1)} %get-tuple-element.14, f32[1,2,64,4096]{3,2,1,0:T(8,128)S(1)} %copy-done, f32[1,2,64,4095]{3,2,1,0:T(8,128)S(1)} %get-tuple-element.43, ...), kind=kLoop, calls=%fused_computation.45 | loop fusion | flops 6291456 | bytes 12648456 | tf_op jit(solution)/shard_map/add | solution.py:122
  14.4 6.2 %copy.65 = f32[1,2,64,4096]{2,1,0,3:T(2,128)} copy(f32[1,2,64,4096]{3,2,1,0:T(8,128)} %get-tuple-element.6) | data formatting | bytes 4194304 | tf_op jit(solution)/shard_map/add | solution.py:122
  20.6 8.1 %reshape.430 = f32[8,1,65536]{2,1,0:T(1,128)} reshape(f32[4096,1,2,64]{3,2,1,0:T(2,128)} %bitcast.65) | data formatting | bytes 4194304
  28.7 27.7 %all_to_all.27 = f32[8,1,65536]{2,1,0:T(1,128)} all-to-all(f32[8,1,65536]{2,1,0:T(1,128)} %reshape.430), channel_id=1, replica_groups=mesh['node_0'=2,'node_1'=4,'space_0'=8,'space_1'=2,'space_2'=2] {'node_0..., dimensions={0} | all-to-all | bytes 4194304 | tf_op jit(solution)/shard_map/all_to_all | solution.py:126
  56.4 0.5 broadcast.59
  56.9 8.5 %reduce = f32[8,65536]{1,0:T(8,128)} reduce(f32[8,1,65536]{2,1,0:T(1,128)} %all_to_all.27, f32[]{:T(128)} %broadcast.59), dimensions={1}, to_apply=%all_to_all.20.reduce_sub_computation | reduce | bytes 4194308 | tf_op jit(solution)/shard_map/all_to_all | solution.py:126
  65.4 6.6 %reshape.431 = f32[4096,1,2,64]{3,2,1,0:T(2,128)} reshape(f32[8,65536]{1,0:T(8,128)} %reduce) | data formatting | bytes 4194304
  72.0 4.8 %copy.74 = f32[1,2,64,8,512]{4,3,2,1,0:T(8,128)} copy(f32[1,2,64,8,512]{2,1,4,3,0:T(2,128)} %bitcast.66) | data formatting | bytes 4194304 | tf_op jit(solution)/shard_map/all_to_all | solution.py:126
  76.8 3.4 %fusion.28 = f32[8,2,64,512]{3,0,2,1:T(8,128)S(1)} fusion(f32[8,8,1,1]{1,0,3,2:T(8,128)S(1)} %copy-done.4, f32[1,2,64,8,512]{4,3,2,1,0:T(8,128)} %copy.74), kind=kOutput, calls=%fused_computation.47 | convolution fusion | flops 50331648 | bytes 4194560 | tf_op jit(solution)/shard_map/mj,jsxy->msxy/dot_general | solution.py:123
  80.2 2.5 %copy.67 = f32[8,2,64,512]{3,2,1,0:T(8,128)} copy(f32[8,2,64,512]{3,0,2,1:T(8,128)S(1)} %fusion.28) | data formatting | bytes 4194304 | tf_op jit(solution)/shard_map/mj,jsxy->msxy/dot_general | solution.py:123
  82.7 4.7 %all-to-all-start.1 = ((f32[8,2,64,512]{3,2,1,0:T(8,128)}), f32[8,2,64,512]{3,2,1,0:T(8,128)}, u32[]{:S(2)}, u32[]{:S(2)}) async-start(f32[8,2,64,512]{3,2,1,0:T(8,128)} %copy.67), calls=%async_computation.1 | async-start | bytes 4194304 | tf_op jit(solution)/shard_map/all_to_all | solution.py:129
  87.4 0.6 dynamic_slice.3
  88.7 25.6 %all-to-all-done.1 = f32[8,2,64,512]{3,2,1,0:T(8,128)} async-done(((f32[8,2,64,512]{3,2,1,0:T(8,128)}), f32[8,2,64,512]{3,2,1,0:T(8,128)}, u32[]{:S(2)}, u32[]{:S(2)}) %all-to-all-start.1) | async-done | bytes 2097184 | tf_op jit(solution)/shard_map/all_to_all | solution.py:129
  114.3 1.8 multiply_bitcast_fusion
  116.2 2.5 %copy.68 = f32[1,2,64,8,512]{4,3,2,1,0:T(8,128)} copy(f32[1,2,64,8,512]{4,2,1,3,0:T(8,128)S(1)} %multiply_bitcast_fusion) | data formatting | bytes 4194304 | tf_op jit(solution)/shard_map/mul | solution.py:130
  118.7 2.7 %mul.127 = f32[2,64,4096]{2,1,0:T(8,128)} reshape(f32[1,2,64,8,512]{4,3,2,1,0:T(8,128)} %copy.68) | data formatting | bytes 4194304 | tf_op jit(solution)/shard_map/mul | solution.py:130
  121.4 4.0 %fusion.32 = (f32[]{:T(128)}, f32[1,1,2,64,4096]{4,3,2,1,0:T(8,128)S(1)}) fusion(f32[1,2,64,4096]{3,2,1,0:T(8,128)S(1)} %copy-done, f32[2,64,4096]{2,1,0:T(8,128)} %param.7, f32[2,64,4096]{2,1,0:T(8,128)} %mul.127, f32[1,2,64,4096]{3,2,1,0:T(8,128)} %get-tuple-element.7, f32[]{:T(128)} %bitcast.13), kind=kLoop, calls=%fused_computation.53 | loop fusion | flops 3145727 | bytes 10485768 | tf_op jit(solution)/shard_map/reduce_max | solution.py:131
  125.5 1.2 copy-done.1
  126.7 0.3 copy.70
  127.0 0.9 collective-permute-start.3
  127.9 1.0 copy.69
  128.9 6.8 %collective-permute-start.2 = (f32[2,1,2,6,4096]{4,2,3,1,0:T(2,128)}, f32[2,1,2,6,4096]{4,2,3,1,0:T(2,128)}, u32[]{:S(2)}, u32[]{:S(2)}) collective-permute-start(f32[2,1,2,6,4096]{4,2,3,1,0:T(2,128)} %copy.69), channel_id=1, source_target_pairs={{0,1},{1,2},{2,3},{3,4},{4,5},{5,6},{6,7},{7,8},{8,9},{9,10},{10,1... | collective-permute-start | bytes 1179656 | tf_op jit(solution)/shard_map/ppermute | solution.py:26
  135.7 9.8 %pmax.35 = f32[]{:T(128)} all-reduce(f32[]{:T(128)} %get-tuple-element.10), channel_id=1, replica_groups=mesh['node_0'=2,'node_1'=4,'space_0'=8,'space_1'=2,'space_2'=2] {'node_0'}, use_global_device_ids=true, to_apply=%region_1.2 | all-reduce | flops 1 | bytes 8 | tf_op jit(solution)/shard_map/pmax | solution.py:34
  145.5 12.7 %pmax.36 = f32[]{:T(128)} all-reduce(f32[]{:T(128)} %pmax.35), channel_id=1, replica_groups=mesh['node_0'=2,'node_1'=4,'space_0'=8,'space_1'=2,'space_2'=2] {'node_1'}, use_global_device_ids=true, to_apply=%region_2.3 | all-reduce | flops 1 | bytes 8 | tf_op jit(solution)/shard_map/pmax | solution.py:34
  158.2 13.1 %pmax.37 = f32[]{:T(128)} all-reduce(f32[]{:T(128)} %pmax.36), channel_id=1, replica_groups=mesh['node_0'=2,'node_1'=4,'space_0'=8,'space_1'=2,'space_2'=2] {'space_0'}, use_global_device_ids=true, to_apply=%region_3.4 | all-reduce | flops 1 | bytes 8 | tf_op jit(solution)/shard_map/pmax | solution.py:34
  171.2 5.9 %pmax.38 = f32[]{:T(128)} all-reduce(f32[]{:T(128)} %pmax.37), channel_id=1, replica_groups=mesh['node_0'=2,'node_1'=4,'space_0'=8,'space_1'=2,'space_2'=2] {'space_1'}, use_global_device_ids=true, to_apply=%region_4.5 | all-reduce | flops 1 | bytes 8 | tf_op jit(solution)/shard_map/pmax | solution.py:34
  177.1 7.4 %pmax.39 = f32[]{:T(128)} all-reduce(f32[]{:T(128)} %pmax.38), channel_id=1, replica_groups=mesh['node_0'=2,'node_1'=4,'space_0'=8,'space_1'=2,'space_2'=2] {'space_2'}, use_global_device_ids=true, to_apply=%region_5.6 | all-reduce | flops 1 | bytes 8 | tf_op jit(solution)/shard_map/pmax | solution.py:34
  184.6 0.2 copy.72
  184.8 1.2 copy.71
  186.1 2.3 %pad_maximum_fusion = f32[2,1,2,76,4096]{4,3,2,1,0:T(8,128)S(1)} fusion(f32[2,1,2,6,4096]{4,3,2,1,0:T(8,128)S(1)} %copy.72, f32[1,1,2,64,4096]{4,3,2,1,0:T(8,128)} %copy-done.1, f32[1,1,2,64,4096]{4,3,2,1,0:T(8,128)S(1)} %bitcast.64, f32[2,1,2,6,4096]{4,3,2,1,0:T(8,128)S(1)} %copy.71), kind=kLoop, calls=%fused_computation | loop fusion | flops 3735552 | bytes 9961472 | tf_op jit(solution)/shard_map/concatenate | solution.py:28
  188.4 0.6 slice_bitcast_fusion.1
  189.1 1.0 fusion.42
  190.0 1.8 fusion.3
  192.0 0.9 fusion.40
  192.9 1.1 fusion.19
  194.0 0.8 fusion.50
  194.9 1.1 fusion.15
  196.1 0.8 fusion.48
  196.9 1.1 fusion.11
  198.1 0.8 fusion.46
  199.0 1.1 fusion.7
  200.2 0.8 fusion.44
  201.0 2.4 %fusion.23 = f32[1,2,64,4096]{3,2,1,0:T(8,128)} fusion(f32[1,2,66,4096]{3,2,1,0:T(8,128)S(1)} %fusion.7, f32[1,2,76,4096]{3,2,1,0:T(8,128)S(1)} %get-tuple-element.8, f32[1,2,64,1]{3,2,1,0:T(8,128)S(1)} %get-tuple-element.25, f32[1,2,64,4095]{3,2,1,0:T(8,128)S(1)} %get-tuple-element.27, f32[1,2,64,4095]{3,2,1,0:T(8,128)S(1)} %get-tuple-element.26, ...), kind=kLoop, calls=%fused_computation.37 | loop fusion | flops 4194304 | bytes 12582928 | tf_op jit(solution)/shard_map/div | solution.py:145
  (30 shorter events, 1.1 us)
Async XLA Ops:
  1.7 8.3 %collective-permute-start.1 = (f32[1,2,1,4096]{3,1,2,0:T(2,128)S(1)}, f32[1,2,1,4096]{3,1,2,0:T(2,128)S(1)}, u32[]{:S(2)}, u32[]{:S(2)}) collective-permute-start(f32[1,2,1,4096]{3,1,2,0:T(2,128)S(1)} %copy.76), channel_id=1, source_target_pairs={{0,1},{1,2},{2,3},{3,4},{4,5},{5,6},{6,7},{7,8},{8,9},{9,10},{10,1... | collective-permute-start | bytes 98312 | tf_op jit(solution)/shard_map/ppermute | solution.py:26
  6.1 3.2 %copy-start = (f32[1,2,64,4096]{3,2,1,0:T(8,128)S(1)}, f32[1,2,64,4096]{3,2,1,0:T(8,128)}, u32[]{:S(2)}) copy-start(f32[1,2,64,4096]{3,2,1,0:T(8,128)} %param.8) | copy-start | bytes 6291460
  6.2 3.2 %copy-start.2 = (f32[64,4096]{1,0:T(8,128)S(1)}, f32[64,4096]{1,0:T(8,128)}, u32[]{:S(2)}) copy-start(f32[64,4096]{1,0:T(8,128)} %param.9) | copy-start | bytes 3145732
  6.2 3.4 %copy-start.3 = (f32[64,4096]{1,0:T(8,128)S(1)}, f32[64,4096]{1,0:T(8,128)}, u32[]{:S(2)}) copy-start(f32[64,4096]{1,0:T(8,128)} %param.10) | copy-start | bytes 3145732
  6.2 5.2 %collective-permute-start = (f32[1,2,1,4096]{3,1,2,0:T(2,128)S(1)}, f32[1,2,1,4096]{3,1,2,0:T(2,128)S(1)}, u32[]{:S(2)}, u32[]{:S(2)}) collective-permute-start(f32[1,2,1,4096]{3,1,2,0:T(2,128)S(1)} %copy.75), channel_id=1, source_target_pairs={{1,0},{2,1},{3,2},{4,3},{5,4},{6,5},{7,6},{8,7},{9,8},{10,9},{11,1... | collective-permute-start | bytes 98312 | tf_op jit(solution)/shard_map/ppermute | solution.py:27
  9.6 1.9 copy-start.5
  72.0 4.8 %copy-start.4 = (f32[8,8,1,1]{1,0,3,2:T(8,128)S(1)}, f32[8,8,1,1]{1,0,3,2:T(8,128)}, u32[]{:S(2)}) copy-start(f32[8,8,1,1]{1,0,3,2:T(8,128)} %constant.38) | copy-start | bytes 772
  82.7 4.7 %copy-start.6 = (f32[8]{0:T(128)S(1)}, f32[8]{0:T(128)}, u32[]{:S(2)}) copy-start(f32[8]{0:T(128)} %constant.34.clone) | copy-start | bytes 100
  82.7 31.6 %all-to-all-start.1 = ((f32[8,2,64,512]{3,2,1,0:T(8,128)}), f32[8,2,64,512]{3,2,1,0:T(8,128)}, u32[]{:S(2)}, u32[]{:S(2)}) async-start(f32[8,2,64,512]{3,2,1,0:T(8,128)} %copy.67), calls=%async_computation.1 | async-start | bytes 4194304 | tf_op jit(solution)/shard_map/all_to_all | solution.py:129
  125.4 1.3 copy-start.1
  127.0 57.6 %collective-permute-start.3 = (f32[2,1,2,6,4096]{4,2,3,1,0:T(2,128)S(1)}, f32[2,1,2,6,4096]{4,2,3,1,0:T(2,128)S(1)}, u32[]{:S(2)}, u32[]{:S(2)}) collective-permute-start(f32[2,1,2,6,4096]{4,2,3,1,0:T(2,128)S(1)} %copy.70), channel_id=1, source_target_pairs={{1,0},{2,1},{3,2},{4,3},{5,4},{6,5},{7,6},{8,7},{9,8},{10,9},{11,1... | collective-permute-start | bytes 1179656 | tf_op jit(solution)/shard_map/ppermute | solution.py:27
  128.9 55.9 %collective-permute-start.2 = (f32[2,1,2,6,4096]{4,2,3,1,0:T(2,128)}, f32[2,1,2,6,4096]{4,2,3,1,0:T(2,128)}, u32[]{:S(2)}, u32[]{:S(2)}) collective-permute-start(f32[2,1,2,6,4096]{4,2,3,1,0:T(2,128)} %copy.69), channel_id=1, source_target_pairs={{0,1},{1,2},{2,3},{3,4},{4,5},{5,6},{6,7},{7,8},{8,9},{9,10},{10,1... | collective-permute-start | bytes 1179656 | tf_op jit(solution)/shard_map/ppermute | solution.py:26
where the time goes:
time: 204 us; the launch traced here: 203 us
  blocking collectives  76.5 us (38%)
  local copies, waits for them, and re-layouts  49.5 us (24%)
  other arithmetic  28.7 us (14%)
  waiting for transfers between devices  27 us (13%)
  starting transfers between devices  16.8 us (8%)
  matrix products  3.38 us (2%)
    pmax x5, blocking collectives, one_axis_at_a_time(): array = lax.pmax(array, axis)  48.8 us
    all_to_all x1, blocking collectives, shards(): lax.all_to_all(slopes, NODE, split_axis=3, concat_axis=0, tiled=True)  27.7 us
    all_to_all x1, waiting for transfers between devices, shards(): lax.all_to_all(mixed, NODE, split_axis=0, concat_axis=3, tiled=True)  25.6 us
    unnamed x18, local copies, waits for them, and re-layouts  16.2 us
    ppermute x2, starting transfers between devices, padded_2(): before = lax.ppermute(last, axis, up)  11.2 us
    slice x14, local copies, waits for them, and re-layouts, column_pair(): return jnp.roll(field, -1, 3) + jnp.roll(field, 1, 3)  8.86 us
    div x6, other arithmetic, shards(): iterate = (side_here + coupling * beside_all) / divisor  8.62 us
    all_to_all x1, other arithmetic, shards(): lax.all_to_all(slopes, NODE, split_axis=3, concat_axis=0, tiled=True)  8.54 us
  transfers between devices with their start and end apart: 5, of which 2 were waited for; matrix products, arithmetic and copies ran while one was open for 3% of the time, Pallas kernels for 0%

commit v1 on v0

v1 whole, which is shorter than its diff:
```python
import functools

import jax
import jax.numpy as jnp
import numpy as np
from jax import lax
from jax.experimental import pallas as pl
from jax.experimental.pallas import tpu as pltpu
from jax.sharding import PartitionSpec as P

SWEEPS = 6
STEP_SIZE = 4.0
DIFFUSIVITY = (1.0, 0.5)
MESH = pl.DeviceIdType.MESH

TILES = 8
BLOCKS = 32
ROWS = 80
ORDER = (1, 6, 0, 7, 2, 5, 3, 4)
LAST = ORDER[-1]
GROUP = 16


def radau_target(order, value):
    before = 1.0
    current = value
    previous = 1.0
    for degree in range(1, order):
        following = ((2 * degree + 1) * value * current - degree * before) / (degree + 1)
        before = current
        current = following
    previous = before
    return current - previous


@functools.lru_cache(maxsize=None)
def radau_table(total):
    grid_count = 20000
    roots_found = []
    left_value = -1.0
    left_target = radau_target(total, left_value)
    for step_index in range(1, grid_count):
        right_value = -1.0 + 2.0 * step_index / grid_count
        right_target = radau_target(total, right_value)
        if left_target * right_target < 0.0:
            lower = left_value
            upper = right_value
            lower_target = left_target
            for _ in range(80):
                halfway = 0.5 * (lower + upper)
                halfway_target = radau_target(total, halfway)
                if lower_target * halfway_target <= 0.0:
                    upper = halfway
                else:
                    lower = halfway
                    lower_target = halfway_target
            roots_found.append(0.5 * (lower + upper))
        left_value = right_value
        left_target = right_target
    roots_found.append(1.0)
    points = [(value + 1.0) / 2.0 for value in roots_found]
    quad_rows = []
    for node_index in range(total):
        row_values = []
        for basis_index in range(total):
            coefs = [1.0]
            for other_index in range(total):
                if other_index != basis_index:
                    scale = 1.0 / (points[basis_index] - points[other_index])
                    shifted = [0.0] + coefs
                    widened = coefs + [0.0]
                    coefs = [
                        (shifted[k] - points[other_index] * widened[k]) * scale
                        for k in range(len(shifted))
                    ]
            integral = 0.0
            for power_index in range(len(coefs)):
                integral += (
                    coefs[power_index] * points[node_index] ** (power_index + 1) / (power_index + 1)
                )
            row_values.append(integral)
        quad_rows.append(row_values)
    return (np.array(points, np.float32), np.array(quad_rows, np.float32))


def kernel(
    sec_hbm, init_hbm, feed_hbm, kill_hbm,
    out, res_out,
    levels, init, feed, kill, slopes, gathered, mixed, summed, drift, right, partial,
    halo_out, halo_in, edge_out, edge_in, top, top_in, best, best_in,
    load_sem, field_sem,
    slope_send, slope_recv, mixed_send, mixed_recv,
    halo_send, halo_recv, edge_send, edge_recv,
    top_send, top_recv, best_send, best_recv, known_sem,
):
    node = lax.axis_index("node")
    space = lax.axis_index("space")
    points, quad = radau_table(8)

    def per_node(values):
        chosen = jnp.float32(values[0])
        for index in range(1, 8):
            chosen = jnp.where(node == index, jnp.float32(values[index]), chosen)
        return chosen

    steps = np.float32(STEP_SIZE) * points
    couplings = [steps * np.float32(d) for d in DIFFUSIVITY]
    divisors = [np.float32(4.0) * c + np.float32(1.0) for c in couplings]
    node_step = per_node(steps)
    inverse = [per_node((1.0 / d.astype(np.float64)).astype(np.float32)) for d in divisors]
    ratio = [
        per_node((c.astype(np.float64) / d.astype(np.float64)).astype(np.float32))
        for c, d in zip(couplings, divisors)
    ]

    def node_peer(i):
        y, x = node // 4, node % 4
        return (((y + i // 4) % 2) * 4 + (x + i % 4) % 4, space)

    def node_index(i):
        return node_peer(i)[0]

    def plane_peer(j):
        return (node_index(j % 8), (space // 4) * 4 + (space % 4 + j // 8) % 4)

    def deep_peer(i):
        return (node, (space // 4 + i) % 8 * 4 + space % 4)

    def next_peer(i):
        return (node, (space + i + 32) % 32)

    barrier = pltpu.get_barrier_semaphore()
    greeted = (
        [node_peer(i) for i in range(1, 8)]
        + [plane_peer(8 * i) for i in range(1, 4)]
        + [deep_peer(1), deep_peer(7), next_peer(1), next_peer(-1)]
    )
    loads = []
    for t in range(TILES):
        for s in range(2):
            loads.append(pltpu.make_async_copy(
                sec_hbm.at[s, t], levels.at[0, s, :, pl.ds(8 + 8 * t, 8), :], load_sem.at[t, s]
            ))
    fields = [
        pltpu.make_async_copy(feed_hbm, feed, field_sem.at[0]),
        pltpu.make_async_copy(kill_hbm, kill, field_sem.at[1]),
        pltpu.make_async_copy(init_hbm, init, field_sem.at[2]),
    ]
    for copy in loads:
        copy.start()
    for copy in fields:
        copy.start()
    for peer in greeted:
        pl.semaphore_signal(barrier, inc=1, device_id=peer, device_id_type=MESH)

    lane = lax.broadcasted_iota(jnp.int32, (8, 128), 1)
    row = lax.broadcasted_iota(jnp.int32, (8, 128), 0)

    def beside(before, centre, after):
        left = pltpu.roll(jnp.where(lane == 127, before, centre), 1, 1)
        rightward = pltpu.roll(jnp.where(lane == 0, after, centre), 127, 1)
        return rightward + left

    def centres(load, first, count):
        blocks = [(first + BLOCKS - 1) % BLOCKS]
        blocks += [first + i for i in range(count)]
        blocks += [(first + count) % BLOCKS]
        return [load(b) for b in blocks]

    for copy in loads:
        copy.wait()

    for s in range(2):
        flat = levels.at[0, s].reshape(BLOCKS * ROWS, 128)
        halo_out[0, s] = flat[pl.ds(8, BLOCKS, stride=ROWS), :]
        halo_out[1, s] = flat[pl.ds(71, BLOCKS, stride=ROWS), :]
    for copy in fields:
        copy.wait()

    def slope_tile(t):
        base = 8 + 8 * t

        def body(d, carry):
            first = d * 4
            found = []
            for s in range(2):
                line = centres(lambda b: levels[0, s, b, pl.ds(base, 8), :], first, 4)
                laps = []
                for q in range(4):
                    up = levels[0, s, first + q, pl.ds(base - 1, 8), :]
                    down = levels[0, s, first + q, pl.ds(base + 1, 8), :]
                    around = (down + up) + beside(line[q], line[q + 1], line[q + 2])
                    laps.append((line[q + 1], around - 4.0 * line[q + 1]))
                found.append(laps)
            for q in range(4):
                u, lap_u = found[0][q]
                v, lap_v = found[1][q]
                lap_v = 0.5 * lap_v
                grow = feed[t, first + q]
                both = grow + kill[t, first + q]
                product = u * v * v
                slopes[t, d, 0, q] = lap_u + (grow * (1.0 - u) - product)
                slopes[t, d, 1, q] = lap_v + (product - both * v)
                drift[t, d, 0, q] = node_step * lap_u
                drift[t, d, 1, q] = node_step * lap_v
            return carry

        lax.fori_loop(0, 8, body, 0)

    def exchange(source, target, t, send_sem, recv_sem):
        copies = []
        for i in range(1, 8):
            copy = pltpu.make_async_remote_copy(
                source.at[t, node_index(i)], target.at[t, node],
                send_sem, recv_sem.at[t], device_id=node_peer(i), device_id_type=MESH,
            )
            copy.start()
        target[t, node] = source[t, node]

    def arrived(target, t, recv_sem):
        part = target.at[t, pl.ds(0, 7)]
        pltpu.make_async_copy(part, part, recv_sem.at[t]).wait()

    def mix_tile(t):
        def body(piece, carry):
            s, q = piece // 4, piece % 4
            values = [gathered[t, j, s, q] for j in range(8)]
            for m in range(8):
                total = values[0] * float(STEP_SIZE * quad[m, 0])
                for j in range(1, 8):
                    total = total + values[j] * float(STEP_SIZE * quad[m, j])
                mixed[t, m, s, q] = total
            return carry

        lax.fori_loop(0, 8, body, 0)

    def right_tile(t, biggest):
        base = 8 + 8 * t

        def body(d, carry):
            for s in range(2):
                for q in range(4):
                    block = d * 4 + q
                    value = init[s, t, block] + summed[t, d, s, q]
                    here = levels[0, s, block, pl.ds(base, 8), :]
                    carry = jnp.maximum(carry, jnp.abs(value - here))
                    right[t + 1, s, block] = (value - drift[t, d, s, q]) * inverse[s]
            return carry

        return lax.fori_loop(0, 8, body, biggest)

    def sweep(level, t, extra=None):
        base = 8 + 8 * t
        for s in range(2):
            def body(g, carry):
                first = g * GROUP
                line = centres(lambda b: levels[level - 1, s, b, pl.ds(base, 8), :], first, GROUP)
                for i in range(GROUP):
                    block = first + i
                    up = levels[level - 1, s, block, pl.ds(base - 1, 8), :]
                    down = levels[level - 1, s, block, pl.ds(base + 1, 8), :]
                    around = (down + up) + beside(line[i], line[i + 1], line[i + 2])
                    if extra is not None:
                        beyond = jnp.broadcast_to(
                            edge_in[extra, level - 2, s, pl.ds(block, 1), :], (8, 128)
                        )
                        around = around + jnp.where(row == 7 * extra, beyond, 0.0)
                    value = right[t + 1, s, block] + ratio[s] * around
                    if isinstance(level, int) and level == SWEEPS:
                        out[s, t, block] = value
                    else:
                        levels[level, s, block, pl.ds(base, 8), :] = value
                return carry

            lax.fori_loop(0, BLOCKS // GROUP, body, 0)

    def response(level, t, extra):
        base = 8 if extra == 0 else 64
        beyond = 0 if extra == 0 else 72
        for s in range(2):
            def body(g, carry):
                first = g * GROUP
                if level == 1:
                    for i in range(GROUP):
                        near = levels[0, s, first + i, pl.ds(base + (-7 if extra == 0 else 7), 8), :]
                        levels[1, s, first + i, pl.ds(beyond, 8), :] = jnp.where(
                            row == (7 if extra == 0 else 0), ratio[s] * near, 0.0
                        )
                    return carry
                line = centres(lambda b: levels[level - 1, s, b, pl.ds(beyond, 8), :], first, GROUP)
                for i in range(GROUP):
                    block = first + i
                    if extra == 0:
                        down = levels[level - 1, s, block, pl.ds(beyond + 1, 8), :]
                        up = jnp.where(row == 0, 0.0, pltpu.roll(line[i + 1], 1, 0))
                    else:
                        up = levels[level - 1, s, block, pl.ds(beyond - 1, 8), :]
                        down = jnp.where(row == 7, 0.0, pltpu.roll(line[i + 1], 7, 0))
                    around = (down + up) + beside(line[i], line[i + 1], line[i + 2])
                    levels[level, s, block, pl.ds(beyond, 8), :] = ratio[s] * around
                return carry

            lax.fori_loop(0, BLOCKS // GROUP, body, 0)

    def send_edges():
        for e, t in ((0, 0), (1, 7)):
            for s in range(2):
                for k in range(1, SWEEPS):
                    def body(g, carry):
                        first = g * GROUP
                        if k == 1:
                            load = lambda b: levels[0, s, b, pl.ds(8 + 8 * t, 8), :]
                        else:
                            load = lambda b: partial[(k - 1) % 2, e, s, b]
                        line = centres(load, first, GROUP)
                        for i in range(GROUP):
                            centre = line[i + 1]
                            up = jnp.where(row == 0, 0.0, pltpu.roll(centre, 1, 0))
                            down = jnp.where(row == 7, 0.0, pltpu.roll(centre, 7, 0))
                            around = (down + up) + beside(line[i], centre, line[i + 2])
                            partial[k % 2, e, s, first + i] = (
                                right[t + 1, s, first + i] + ratio[s] * around
                            )
                        return carry

                    lax.fori_loop(0, BLOCKS // GROUP, body, 0)
                    flat = partial.at[k % 2, e, s].reshape(BLOCKS * 8, 128)
                    edge_out[e, k - 1, s] = flat[pl.ds(7 * e, BLOCKS, stride=8), :]

    def side_copies(source, target, send_sem, recv_sem):
        return [
            pltpu.make_async_remote_copy(
                source.at[e], target.at[1 - e], send_sem.at[e], recv_sem.at[1 - e],
                device_id=next_peer(2 * e - 1), device_id_type=MESH,
            )
            for e in range(2)
        ]

    halo_copies = side_copies(halo_out, halo_in, halo_send, halo_recv)
    edge_copies = side_copies(edge_out, edge_in, edge_send, edge_recv)

    slope_tile(ORDER[0])
    pl.semaphore_wait(barrier, len(greeted))
    for copy in halo_copies:
        copy.start()
    exchange(slopes, gathered, ORDER[0], slope_send, slope_recv)
    for peer in [plane_peer(8 * i) for i in range(1, 4)] + [deep_peer(1), deep_peer(7)]:
        pl.semaphore_signal(known_sem.at[0], inc=1, device_id=peer, device_id_type=MESH)
    slope_tile(ORDER[1])
    exchange(slopes, gathered, ORDER[1], slope_send, slope_recv)
    for copy in halo_copies:
        copy.wait_recv()
    for s in range(2):
        flat = levels.at[0, s].reshape(BLOCKS * ROWS, 128)
        flat[pl.ds(7, BLOCKS, stride=ROWS), :] = halo_in[0, s]
        flat[pl.ds(72, BLOCKS, stride=ROWS), :] = halo_in[1, s]
    for t in ORDER[2:]:
        slope_tile(t)
        exchange(slopes, gathered, t, slope_send, slope_recv)
    pl.semaphore_wait(known_sem.at[0], 5)
    for i in (2, 6):
        pl.semaphore_signal(known_sem.at[1], inc=1, device_id=deep_peer(i), device_id_type=MESH)

    for t in ORDER:
        arrived(gathered, t, slope_recv)
        mix_tile(t)
        exchange(mixed, summed, t, mixed_send, mixed_recv)
    pl.semaphore_wait(known_sem.at[1], 2)

    biggest = jnp.zeros((8, 128), jnp.float32)
    for t in ORDER[:-1]:
        arrived(summed, t, mixed_recv)
        biggest = right_tile(t, biggest)
        if t == ORDER[3]:
            send_edges()
            for copy in edge_copies:
                copy.start()

    def sweep_range(low, high):
        def one_level(level, carry):
            lax.fori_loop(low, high, lambda t, c: (sweep(level, t), c)[1], 0)
            return carry

        lax.fori_loop(1, SWEEPS, one_level, 0)

    def last_level(low, high):
        lax.fori_loop(low, high, lambda t, c: (sweep(SWEEPS, t), c)[1], 0)

    def early_level(level, carry):
        def one(i, c):
            t = i + (i + (TILES - 1 - LAST)) // (TILES - 1)
            sweep(level, t)
            return c

        lax.fori_loop(0, TILES - 1, one, 0)
        return carry

    lax.fori_loop(1, SWEEPS, early_level, 0)
    last_level(1, LAST - 1)
    last_level(LAST + 2, TILES - 1)

    arrived(summed, LAST, mixed_recv)
    biggest = right_tile(LAST, biggest)
    top[...] = jnp.max(biggest, axis=0, keepdims=True)
    top_copies = []
    for j in range(1, 32):
        copy = pltpu.make_async_remote_copy(
            top, top_in.at[j], top_send.at[j], top_recv.at[j],
            device_id=plane_peer(j), device_id_type=MESH,
        )
        copy.start()
        top_copies.append(copy)
    top_in[0] = top[...]

    sweep_range(LAST - 1, LAST + 2)
    last_level(LAST - 1, LAST + 2)

    for copy in top_copies:
        copy.wait_recv()
    best[...] = jnp.max(top_in[...], axis=0)
    best_copies = []
    for i in range(1, 8):
        copy = pltpu.make_async_remote_copy(
            best, best_in.at[i], best_send.at[i], best_recv.at[i],
            device_id=deep_peer(i), device_id_type=MESH,
        )
        copy.start()
        best_copies.append(copy)
    best_in[0] = best[...]

    for copy in edge_copies:
        copy.wait_recv()
    for level in range(1, SWEEPS + 1):
        for e, t in ((0, 0), (1, 7)):
            if level > 1:
                sweep(level, t, extra=e)
            if level < SWEEPS:
                response(level, -1 if e == 0 else 8, e)

    for copy in best_copies:
        copy.wait_recv()
    res_out[0, 0] = jnp.max(best_in[...])

    for source, sem in ((slopes, slope_send), (mixed, mixed_send)):
        part = source.at[:, pl.ds(0, 7)]
        pltpu.make_async_copy(part, part, sem).wait()
    for copy in halo_copies + edge_copies + top_copies + best_copies:
        copy.wait_send()


def shards(initial, sections, feed_rate, kill_rate):
    def tiled(array):
        lead = array.shape[:-2]
        n = len(lead)
        split = array.reshape(lead + (TILES, 8, BLOCKS, 128))
        return jnp.swapaxes(split, n + 1, n + 2)

    f32 = jnp.float32
    whole = (2, TILES, BLOCKS, 8, 128)
    parts = (TILES, 8, 2, 4, 8, 128)
    dma = pltpu.SemaphoreType.DMA
    out, biggest = pl.pallas_call(
        kernel,
        out_shape=(
            jax.ShapeDtypeStruct(whole, f32),
            jax.ShapeDtypeStruct((1, 1), f32),
        ),
        in_specs=[pl.BlockSpec(memory_space=pl.ANY)] * 4,
        out_specs=(pl.BlockSpec(memory_space=pltpu.VMEM), pl.BlockSpec(memory_space=pltpu.SMEM)),
        scratch_shapes=[
            pltpu.VMEM((SWEEPS, 2, BLOCKS, ROWS, 128), f32),
            pltpu.VMEM(whole, f32),
            pltpu.VMEM(whole[1:], f32),
            pltpu.VMEM(whole[1:], f32),
            pltpu.VMEM(parts, f32),
            pltpu.VMEM(parts, f32),
            pltpu.VMEM(parts, f32),
            pltpu.VMEM(parts, f32),
            pltpu.VMEM(parts, f32),
            pltpu.VMEM((TILES + 2, 2, BLOCKS, 8, 128), f32),
            pltpu.VMEM((2, 2, 2, BLOCKS, 8, 128), f32),
            pltpu.VMEM((2, 2, BLOCKS, 128), f32),
            pltpu.VMEM((2, 2, BLOCKS, 128), f32),
            pltpu.VMEM((2, SWEEPS - 1, 2, BLOCKS, 128), f32),
            pltpu.VMEM((2, SWEEPS - 1, 2, BLOCKS, 128), f32),
            pltpu.VMEM((1, 128), f32),
            pltpu.VMEM((32, 1, 128), f32),
            pltpu.VMEM((1, 128), f32),
            pltpu.VMEM((8, 1, 128), f32),
            dma((TILES, 2)),
            dma((3,)),
            dma,
            dma((TILES,)),
            dma,
            dma((TILES,)),
            dma((2,)),
            dma((2,)),
            dma((2,)),
            dma((2,)),
            dma((32,)),
            dma((32,)),
            dma((8,)),
            dma((8,)),
            pltpu.SemaphoreType.REGULAR((2,)),
        ],
        compiler_params=pltpu.CompilerParams(
            collective_id=0, has_side_effects=True, vmem_limit_bytes=56 * 1024 * 1024
        ),
    )(tiled(sections[0]), tiled(initial), tiled(feed_rate), tiled(kill_rate))
    new = jnp.swapaxes(out, 2, 3).reshape(sections.shape)
    return (new, biggest.reshape(()))


def solution(mesh):
    return jax.shard_map(
        shards,
        mesh=mesh,
        in_specs=(
            P(None, "space", None),
            P("node", None, "space", None),
            P("space", None),
            P("space", None),
        ),
        out_specs=(P("node", None, "space", None), P()),
        check_vma=False,
    )
```

time: 204 us -> 110 us (0.54)
  the two profiles are of different devices: /device:TPU:1 before, /device:TPU:4 now
where the time goes in v1:
time: 110 us; the launch traced here: 109 us
  Pallas kernels  104 us (95%)
  local copies, waits for them, and re-layouts  3.11 us (3%)
  between operations  2.38 us (2%)
    pallas_call x1, Pallas kernels, shards(): pl.pallas_call(kernel, out_shape=(jax.ShapeDtypeStruct(whole, f32), jax.S...  104 us
    unnamed x1, local copies, waits for them, and re-layouts  3.11 us

profile of v1, /device:TPU:4, one launch (start us, length us, event | category | flops | bytes accessed | tf_op | source)
XLA Modules:
  0.0 109.5 jit_solution(16849926345412991772)
XLA Ops:
  0.6 104.0 %shard_map.59 = (f32[2,8,32,8,128]{4,3,2,1,0:T(8,128)}, f32[1,1]{1,0:T(1,128)}) custom-call(f32[2,8,32,8,128]{4,3,2,1,0:T(8,128)} %bitcast.16, f32[2,8,32,8,128]{4,3,2,1,0:T(8,128)} %bitcast.17, f32[8,32,8,128]{3,2,1,0:T(8,128)} %bitcast.19, f32[8,32,8,128]{3,2,1,0:T(8,128)} %bitcast.20), custom_call_target="tpu_custom_call" | custom-call | tf_op jit(solution)/shard_map/pallas_call | solution.py:462
  104.6 3.1 %copy.8 = f32[1,2,64,4096]{3,2,1,0:T(8,128)} copy(f32[1,2,64,4096]{3,2,1,0:T(8,128)} %bitcast.18) | data formatting | bytes 4194304

commit v2 on v1

--- a/solution.py
+++ b/solution.py
@@ -15,9 +15,9 @@
 
 TILES = 8
 BLOCKS = 32
-ROWS = 80
-ORDER = (1, 6, 0, 7, 2, 5, 3, 4)
-LAST = ORDER[-1]
+ROWS = 104
+FIRST = 16
+ORDER = (1, 6, 0, 7, 5, 4, 3, 2)
 GROUP = 16
 
 
@@ -88,7 +88,7 @@
     out, res_out,
     levels, init, feed, kill, slopes, gathered, mixed, summed, drift, right, partial,
     halo_out, halo_in, edge_out, edge_in, top, top_in, best, best_in,
-    load_sem, field_sem,
+    load_sem, field_sem, init_sem,
     slope_send, slope_recv, mixed_send, mixed_recv,
     halo_send, halo_recv, edge_send, edge_recv,
     top_send, top_recv, best_send, best_recv, known_sem,
@@ -137,21 +137,46 @@
     )
     loads = []
     for t in range(TILES):
-        for s in range(2):
-            loads.append(pltpu.make_async_copy(
-                sec_hbm.at[s, t], levels.at[0, s, :, pl.ds(8 + 8 * t, 8), :], load_sem.at[t, s]
-            ))
+        loads.append([
+            pltpu.make_async_copy(
+                sec_hbm.at[s, t], levels.at[0, s, :, pl.ds(FIRST + 8 * t, 8), :], load_sem.at[t, s]
+            )
+            for s in range(2)
+        ])
     fields = [
-        pltpu.make_async_copy(feed_hbm, feed, field_sem.at[0]),
-        pltpu.make_async_copy(kill_hbm, kill, field_sem.at[1]),
-        pltpu.make_async_copy(init_hbm, init, field_sem.at[2]),
+        [
+            pltpu.make_async_copy(feed_hbm.at[t], feed.at[t], field_sem.at[t, 0]),
+            pltpu.make_async_copy(kill_hbm.at[t], kill.at[t], field_sem.at[t, 1]),
+        ]
+        for t in range(TILES)
     ]
-    for copy in loads:
-        copy.start()
-    for copy in fields:
-        copy.start()
+    init_load = pltpu.make_async_copy(init_hbm, init, init_sem)
+    started, waited = set(), set()
+
+    def start_loads(t):
+        for near in (t - 1, t, t + 1):
+            if 0 <= near < TILES and near not in started:
+                started.add(near)
+                for copy in loads[near]:
+                    copy.start()
+        for copy in fields[t]:
+            copy.start()
+
+    def wait_loads(t):
+        for near in (t - 1, t, t + 1):
+            if 0 <= near < TILES and near not in waited:
+                waited.add(near)
+                for copy in loads[near]:
+                    copy.wait()
+        for copy in fields[t]:
+            copy.wait()
+
+    start_loads(ORDER[0])
     for peer in greeted:
         pl.semaphore_signal(barrier, inc=1, device_id=peer, device_id_type=MESH)
+    for t in ORDER[1:]:
+        start_loads(t)
+    init_load.start()
 
     lane = lax.broadcasted_iota(jnp.int32, (8, 128), 1)
     row = lax.broadcasted_iota(jnp.int32, (8, 128), 0)
@@ -167,18 +192,8 @@
         blocks += [(first + count) % BLOCKS]
         return [load(b) for b in blocks]
 
-    for copy in loads:
-        copy.wait()
-
-    for s in range(2):
-        flat = levels.at[0, s].reshape(BLOCKS * ROWS, 128)
-        halo_out[0, s] = flat[pl.ds(8, BLOCKS, stride=ROWS), :]
-        halo_out[1, s] = flat[pl.ds(71, BLOCKS, stride=ROWS), :]
-    for copy in fields:
-        copy.wait()
-
     def slope_tile(t):
-        base = 8 + 8 * t
+        base = FIRST + 8 * t
 
         def body(d, carry):
             first = d * 4
@@ -235,7 +250,7 @@
         lax.fori_loop(0, 8, body, 0)
 
     def right_tile(t, biggest):
-        base = 8 + 8 * t
+        base = FIRST + 8 * t
 
         def body(d, carry):
             for s in range(2):
@@ -249,58 +264,52 @@
 
         return lax.fori_loop(0, 8, body, biggest)
 
-    def sweep(level, t, extra=None):
-        base = 8 + 8 * t
+    def sweep(level, t, side=None):
+        base = pl.multiple_of(FIRST + 8 * t, 8)
         for s in range(2):
-            def body(g, carry):
-                first = g * GROUP
-                line = centres(lambda b: levels[level - 1, s, b, pl.ds(base, 8), :], first, GROUP)
-                for i in range(GROUP):
-                    block = first + i
-                    up = levels[level - 1, s, block, pl.ds(base - 1, 8), :]
-                    down = levels[level - 1, s, block, pl.ds(base + 1, 8), :]
-                    around = (down + up) + beside(line[i], line[i + 1], line[i + 2])
-                    if extra is not None:
-                        beyond = jnp.broadcast_to(
-                            edge_in[extra, level - 2, s, pl.ds(block, 1), :], (8, 128)
-                        )
-                        around = around + jnp.where(row == 7 * extra, beyond, 0.0)
-                    value = right[t + 1, s, block] + ratio[s] * around
-                    if isinstance(level, int) and level == SWEEPS:
-                        out[s, t, block] = value
-                    else:
-                        levels[level, s, block, pl.ds(base, 8), :] = value
-                return carry
-
-            lax.fori_loop(0, BLOCKS // GROUP, body, 0)
-
-    def response(level, t, extra):
-        base = 8 if extra == 0 else 64
-        beyond = 0 if extra == 0 else 72
+            line = centres(lambda b: levels[level - 1, s, b, pl.ds(base, 8), :], 0, BLOCKS)
+            for b in range(BLOCKS):
+                up = levels[level - 1, s, b, pl.ds(base - 1, 8), :]
+                down = levels[level - 1, s, b, pl.ds(base + 1, 8), :]
+                around = (down + up) + beside(line[b], line[b + 1], line[b + 2])
+                if side is not None:
+                    beyond = jnp.broadcast_to(edge_in[side, level - 2, s, pl.ds(b, 1), :], (8, 128))
+                    around = around + jnp.where(row == 7 * side, beyond, 0.0)
+                value = right[t + 1, s, b] + ratio[s] * around
+                if level == SWEEPS:
+                    out[s, t, b] = value
+                else:
+                    levels[level, s, b, pl.ds(base, 8), :] = value
+
+    def response(level, side):
+        base = pl.multiple_of(FIRST - 8 + 72 * side, 8)
         for s in range(2):
-            def body(g, carry):
-                first = g * GROUP
-                if level == 1:
-                    for i in range(GROUP):
-                        near = levels[0, s, first + i, pl.ds(base + (-7 if extra == 0 else 7), 8), :]
-                        levels[1, s, first + i, pl.ds(beyond, 8), :] = jnp.where(
-                            row == (7 if extra == 0 else 0), ratio[s] * near, 0.0
-                        )
-                    return carry
-                line = centres(lambda b: levels[level - 1, s, b, pl.ds(beyond, 8), :], first, GROUP)
-                for i in range(GROUP):
-                    block = first + i
-                    if extra == 0:
-                        down = levels[level - 1, s, block, pl.ds(beyond + 1, 8), :]
-                        up = jnp.where(row == 0, 0.0, pltpu.roll(line[i + 1], 1, 0))
-                    else:
-                        up = levels[level - 1, s, block, pl.ds(beyond - 1, 8), :]
-                        down = jnp.where(row == 7, 0.0, pltpu.roll(line[i + 1], 7, 0))
-                    around = (down + up) + beside(line[i], line[i + 1], line[i + 2])
-                    levels[level, s, block, pl.ds(beyond, 8), :] = ratio[s] * around
-                return carry
-
-            lax.fori_loop(0, BLOCKS // GROUP, body, 0)
+            if level == 1:
+                for b in range(BLOCKS):
+                    near = levels[0, s, b, pl.ds(base + 1 - 2 * side, 8), :]
+                    levels[1, s, b, pl.ds(base, 8), :] = jnp.where(
+                        row == 7 - 7 * side, ratio[s] * near, 0.0
+                    )
+                continue
+            line = centres(lambda b: levels[level - 1, s, b, pl.ds(base, 8), :], 0, BLOCKS)
+            for b in range(BLOCKS):
+                up = levels[level - 1, s, b, pl.ds(base - 1, 8), :]
+                down = levels[level - 1, s, b, pl.ds(base + 1, 8), :]
+                around = (down + up) + beside(line[b], line[b + 1], line[b + 2])
+                levels[level, s, b, pl.ds(base, 8), :] = ratio[s] * around
+
+    def repeat(low, high, run):
+        def body(t, carry):
+            run(t)
+            return carry
+
+        lax.fori_loop(low, high, body, 0)
+
+    def sweep_all(low, high, last_low, last_high):
+        for level in range(1, SWEEPS):
+            repeat(low, high, functools.partial(sweep, level))
+        if last_high > last_low:
+            repeat(last_low, last_high, functools.partial(sweep, SWEEPS))
 
     def send_edges():
         for e, t in ((0, 0), (1, 7)):
@@ -309,7 +318,7 @@
                     def body(g, carry):
                         first = g * GROUP
                         if k == 1:
-                            load = lambda b: levels[0, s, b, pl.ds(8 + 8 * t, 8), :]
+                            load = lambda b: levels[0, s, b, pl.ds(FIRST + 8 * t, 8), :]
                         else:
                             load = lambda b: partial[(k - 1) % 2, e, s, b]
                         line = centres(load, first, GROUP)
@@ -339,11 +348,17 @@
     halo_copies = side_copies(halo_out, halo_in, halo_send, halo_recv)
     edge_copies = side_copies(edge_out, edge_in, edge_send, edge_recv)
 
+    wait_loads(ORDER[0])
     slope_tile(ORDER[0])
     pl.semaphore_wait(barrier, len(greeted))
+    exchange(slopes, gathered, ORDER[0], slope_send, slope_recv)
+    wait_loads(ORDER[1])
+    for s in range(2):
+        flat = levels.at[0, s].reshape(BLOCKS * ROWS, 128)
+        halo_out[0, s] = flat[pl.ds(FIRST, BLOCKS, stride=ROWS), :]
+        halo_out[1, s] = flat[pl.ds(FIRST + 63, BLOCKS, stride=ROWS), :]
     for copy in halo_copies:
         copy.start()
-    exchange(slopes, gathered, ORDER[0], slope_send, slope_recv)
     for peer in [plane_peer(8 * i) for i in range(1, 4)] + [deep_peer(1), deep_peer(7)]:
         pl.semaphore_signal(known_sem.at[0], inc=1, device_id=peer, device_id_type=MESH)
     slope_tile(ORDER[1])
@@ -352,15 +367,17 @@
         copy.wait_recv()
     for s in range(2):
         flat = levels.at[0, s].reshape(BLOCKS * ROWS, 128)
-        flat[pl.ds(7, BLOCKS, stride=ROWS), :] = halo_in[0, s]
-        flat[pl.ds(72, BLOCKS, stride=ROWS), :] = halo_in[1, s]
+        flat[pl.ds(FIRST - 1, BLOCKS, stride=ROWS), :] = halo_in[0, s]
+        flat[pl.ds(FIRST + 64, BLOCKS, stride=ROWS), :] = halo_in[1, s]
     for t in ORDER[2:]:
+        wait_loads(t)
         slope_tile(t)
         exchange(slopes, gathered, t, slope_send, slope_recv)
     pl.semaphore_wait(known_sem.at[0], 5)
     for i in (2, 6):
         pl.semaphore_signal(known_sem.at[1], inc=1, device_id=deep_peer(i), device_id_type=MESH)
 
+    init_load.wait()
     for t in ORDER:
         arrived(gathered, t, slope_recv)
         mix_tile(t)
@@ -368,39 +385,22 @@
     pl.semaphore_wait(known_sem.at[1], 2)
 
     biggest = jnp.zeros((8, 128), jnp.float32)
-    for t in ORDER[:-1]:
+    for index, t in enumerate(ORDER):
         arrived(summed, t, mixed_recv)
         biggest = right_tile(t, biggest)
-        if t == ORDER[3]:
+        if index == 3:
             send_edges()
             for copy in edge_copies:
                 copy.start()
-
-    def sweep_range(low, high):
-        def one_level(level, carry):
-            lax.fori_loop(low, high, lambda t, c: (sweep(level, t), c)[1], 0)
-            return carry
-
-        lax.fori_loop(1, SWEEPS, one_level, 0)
-
-    def last_level(low, high):
-        lax.fori_loop(low, high, lambda t, c: (sweep(SWEEPS, t), c)[1], 0)
-
-    def early_level(level, carry):
-        def one(i, c):
-            t = i + (i + (TILES - 1 - LAST)) // (TILES - 1)
-            sweep(level, t)
-            return c
-
-        lax.fori_loop(0, TILES - 1, one, 0)
-        return carry
-
-    lax.fori_loop(1, SWEEPS, early_level, 0)
-    last_level(1, LAST - 1)
-    last_level(LAST + 2, TILES - 1)
-
-    arrived(summed, LAST, mixed_recv)
-    biggest = right_tile(LAST, biggest)
+        if index == 2:
+            sweep_all(0, 2, 0, 0)
+        if index == 4:
+            sweep_all(5, 8, 6, 7)
+        if index == 5:
+            sweep_all(4, 6, 5, 6)
+        if index == 6:
+            sweep_all(3, 5, 4, 5)
+
     top[...] = jnp.max(biggest, axis=0, keepdims=True)
     top_copies = []
     for j in range(1, 32):
@@ -412,8 +412,7 @@
         top_copies.append(copy)
     top_in[0] = top[...]
 
-    sweep_range(LAST - 1, LAST + 2)
-    last_level(LAST - 1, LAST + 2)
+    sweep_all(1, 4, 1, 4)
 
     for copy in top_copies:
         copy.wait_recv()
@@ -431,11 +430,10 @@
     for copy in edge_copies:
         copy.wait_recv()
     for level in range(1, SWEEPS + 1):
-        for e, t in ((0, 0), (1, 7)):
-            if level > 1:
-                sweep(level, t, extra=e)
-            if level < SWEEPS:
-                response(level, -1 if e == 0 else 8, e)
+        if level > 1:
+            repeat(0, 2, lambda side: sweep(level, 7 * side, side))
+        if level < SWEEPS:
+            repeat(0, 2, functools.partial(response, level))
 
     for copy in best_copies:
         copy.wait_recv()
@@ -462,10 +460,10 @@
     out, biggest = pl.pallas_call(
         kernel,
         out_shape=(
-            jax.ShapeDtypeStruct(whole, f32),
+            pltpu.VMEM(whole, f32),
             jax.ShapeDtypeStruct((1, 1), f32),
         ),
-        in_specs=[pl.BlockSpec(memory_space=pl.ANY)] * 4,
+        in_specs=[pl.BlockSpec(memory_space=pltpu.HBM)] * 4,
         out_specs=(pl.BlockSpec(memory_space=pltpu.VMEM), pl.BlockSpec(memory_space=pltpu.SMEM)),
         scratch_shapes=[
             pltpu.VMEM((SWEEPS, 2, BLOCKS, ROWS, 128), f32),
@@ -488,7 +486,8 @@
             pltpu.VMEM((1, 128), f32),
             pltpu.VMEM((8, 1, 128), f32),
             dma((TILES, 2)),
-            dma((3,)),
+            dma((TILES, 2)),
+            dma,
             dma,
             dma((TILES,)),
             dma,
@@ -504,9 +503,9 @@
             pltpu.SemaphoreType.REGULAR((2,)),
         ],
         compiler_params=pltpu.CompilerParams(
-            collective_id=0, has_side_effects=True, vmem_limit_bytes=56 * 1024 * 1024
+            collective_id=0, has_side_effects=True, vmem_limit_bytes=44 * 1024 * 1024
         ),
-    )(tiled(sections[0]), tiled(initial), tiled(feed_rate), tiled(kill_rate))
+    )(*[pltpu.with_memory_space_constraint(tiled(x), pltpu.HBM) for x in (sections[0], initial, feed_rate, kill_rate)])
     new = jnp.swapaxes(out, 2, 3).reshape(sections.shape)
     return (new, biggest.reshape(()))
 

time: 110 us -> 77.8 us (0.71)
  the two profiles are of different devices: /device:TPU:4 before, /device:TPU:1 now
where the time goes in v2:
time: 77.8 us; the launch traced here: 77.7 us
  Pallas kernels  74.1 us (95%)
  between operations  2.33 us (3%)
  local copies, waits for them, and re-layouts  1.32 us (2%)
    pallas_call x1, Pallas kernels, shards(): pl.pallas_call(kernel, out_shape=(pltpu.VMEM(whole, f32), jax.ShapeDtypeS...  74.1 us

profile of v2, /device:TPU:1, one launch (start us, length us, event | category | flops | bytes accessed | tf_op | source)
XLA Modules:
  0.0 77.7 jit_solution(15165757337944242247)
XLA Ops:
  0.6 74.1 %shard_map.59 = (f32[2,8,32,8,128]{4,3,2,1,0:T(8,128)S(1)}, f32[1,1]{1,0:T(1,128)}) custom-call(f32[2,8,32,8,128]{4,3,2,1,0:T(8,128)} %bitcast.17, f32[2,8,32,8,128]{4,3,2,1,0:T(8,128)} %bitcast.18, f32[8,32,8,128]{3,2,1,0:T(8,128)} %bitcast.19, f32[8,32,8,128]{3,2,1,0:T(8,128)} %bitcast.20), custom_call_target="tpu_custom_call" | custom-call | tf_op jit(solution)/shard_map/pallas_call | solution.py:460
  74.7 1.3 %copy.8 = f32[1,2,64,4096]{3,2,1,0:T(8,128)} copy(f32[1,2,64,4096]{3,2,1,0:T(8,128)S(1)} %bitcast.16) | data formatting | bytes 4194304

commit v3 on v2

--- a/solution.py
+++ b/solution.py
@@ -19,6 +19,8 @@
 FIRST = 16
 ORDER = (1, 6, 0, 7, 5, 4, 3, 2)
 GROUP = 16
+LAG = 2
+AHEAD = 3
 
 
 def radau_target(order, value):
@@ -369,37 +371,47 @@
         flat = levels.at[0, s].reshape(BLOCKS * ROWS, 128)
         flat[pl.ds(FIRST - 1, BLOCKS, stride=ROWS), :] = halo_in[0, s]
         flat[pl.ds(FIRST + 64, BLOCKS, stride=ROWS), :] = halo_in[1, s]
-    for t in ORDER[2:]:
+    def send_slopes(t):
         wait_loads(t)
         slope_tile(t)
         exchange(slopes, gathered, t, slope_send, slope_recv)
+
+    for t in ORDER[2:AHEAD]:
+        send_slopes(t)
     pl.semaphore_wait(known_sem.at[0], 5)
     for i in (2, 6):
         pl.semaphore_signal(known_sem.at[1], inc=1, device_id=deep_peer(i), device_id_type=MESH)
 
     init_load.wait()
-    for t in ORDER:
-        arrived(gathered, t, slope_recv)
-        mix_tile(t)
-        exchange(mixed, summed, t, mixed_send, mixed_recv)
-    pl.semaphore_wait(known_sem.at[1], 2)
-
     biggest = jnp.zeros((8, 128), jnp.float32)
-    for index, t in enumerate(ORDER):
+    for step in range(TILES + LAG):
+        if step < TILES:
+            t = ORDER[step]
+            arrived(gathered, t, slope_recv)
+            mix_tile(t)
+            exchange(mixed, summed, t, mixed_send, mixed_recv)
+            if step + AHEAD < TILES:
+                send_slopes(ORDER[step + AHEAD])
+        index = step - LAG
+        if index < 0:
+            continue
+        t = ORDER[index]
         arrived(summed, t, mixed_recv)
+        if index == 6:
+            for copy in edge_copies:
+                copy.start()
         biggest = right_tile(t, biggest)
+        if index == 2:
+            sweep_all(0, 2, 0, 0)
         if index == 3:
             send_edges()
-            for copy in edge_copies:
-                copy.start()
-        if index == 2:
-            sweep_all(0, 2, 0, 0)
         if index == 4:
             sweep_all(5, 8, 6, 7)
         if index == 5:
             sweep_all(4, 6, 5, 6)
         if index == 6:
             sweep_all(3, 5, 4, 5)
+    pl.semaphore_wait(known_sem.at[1], 2)
 
     top[...] = jnp.max(biggest, axis=0, keepdims=True)
     top_copies = []

time: 77.8 us -> 73.8 us (0.949)
  Pallas kernels: 74.1 us -> 70.1 us
    pallas_call x1, Pallas kernels: 74.1 us -> 70.1 us  [shards(): pl.pallas_call(kernel, out_shape=(pltpu.VMEM(whole, f32), jax.ShapeDtypeS...]
where the time goes in v3:
time: 73.8 us; the launch traced here: 73.7 us
  Pallas kernels  70.1 us (95%)
  between operations  2.33 us (3%)
  local copies, waits for them, and re-layouts  1.32 us (2%)
    pallas_call x1, Pallas kernels, shards(): pl.pallas_call(kernel, out_shape=(pltpu.VMEM(whole, f32), jax.ShapeDtypeS...  70.1 us

profile of v3, /device:TPU:1, one launch (start us, length us, event | category | flops | bytes accessed | tf_op | source)
XLA Modules:
  0.0 73.7 jit_solution(11368801493269155192)
XLA Ops:
  0.6 70.1 %shard_map.59 = (f32[2,8,32,8,128]{4,3,2,1,0:T(8,128)S(1)}, f32[1,1]{1,0:T(1,128)}) custom-call(f32[2,8,32,8,128]{4,3,2,1,0:T(8,128)} %bitcast.17, f32[2,8,32,8,128]{4,3,2,1,0:T(8,128)} %bitcast.18, f32[8,32,8,128]{3,2,1,0:T(8,128)} %bitcast.19, f32[8,32,8,128]{3,2,1,0:T(8,128)} %bitcast.20), custom_call_target="tpu_custom_call" | custom-call | tf_op jit(solution)/shard_map/pallas_call | solution.py:472
  70.7 1.3 %copy.8 = f32[1,2,64,4096]{3,2,1,0:T(8,128)} copy(f32[1,2,64,4096]{3,2,1,0:T(8,128)S(1)} %bitcast.16) | data formatting | bytes 4194304

commit v4 on v3

--- a/solution.py
+++ b/solution.py
@@ -18,7 +18,7 @@
 ROWS = 104
 FIRST = 16
 ORDER = (1, 6, 0, 7, 5, 4, 3, 2)
-GROUP = 16
+GROUP = 32
 LAG = 2
 AHEAD = 3
 

time: 73.8 us -> 73.8 us (level)
  no operation moved by 1% of the time
where the time goes in v4:
time: 73.8 us; the launch traced here: 73.7 us
  Pallas kernels  70.1 us (95%)
  between operations  2.33 us (3%)
  local copies, waits for them, and re-layouts  1.32 us (2%)
    pallas_call x1, Pallas kernels, shards(): pl.pallas_call(kernel, out_shape=(pltpu.VMEM(whole, f32), jax.ShapeDtypeS...  70.1 us

profile of v4, /device:TPU:1, one launch (start us, length us, event | category | flops | bytes accessed | tf_op | source)
XLA Modules:
  0.0 73.7 jit_solution(5904203925246329189)
XLA Ops:
  0.6 70.1 %shard_map.59 = (f32[2,8,32,8,128]{4,3,2,1,0:T(8,128)S(1)}, f32[1,1]{1,0:T(1,128)}) custom-call(f32[2,8,32,8,128]{4,3,2,1,0:T(8,128)} %bitcast.17, f32[2,8,32,8,128]{4,3,2,1,0:T(8,128)} %bitcast.18, f32[8,32,8,128]{3,2,1,0:T(8,128)} %bitcast.19, f32[8,32,8,128]{3,2,1,0:T(8,128)} %bitcast.20), custom_call_target="tpu_custom_call" | custom-call | tf_op jit(solution)/shard_map/pallas_call | solution.py:472
  70.7 1.3 %copy.8 = f32[1,2,64,4096]{3,2,1,0:T(8,128)} copy(f32[1,2,64,4096]{3,2,1,0:T(8,128)S(1)} %bitcast.16) | data formatting | bytes 4194304
